TPU v7x, 32 devices: a whole 2x2x4 slice. The times are simulated.
32 devices in a mesh: seq: 8 (over z, x), head: 4 (over y, core).
Axes of the slice: x: 2, y: 2, z: 4, core: 2. Of those that a mesh axis runs over, the one named last changes fastest.
Arguments:
- hidden: bfloat16 [2048, 4096], P(('seq', 'head')), may hold values from -90 to 90
- block_order: int32 [16], replicated, may hold values from 0 to 15, as said below
- segment_ids: int32 [2048], replicated, may hold values from 0 to 3, never falling along the last dimension, each value on 1 to 1024 neighbouring positions
- w_query: bfloat16 [4096, 4096], P(None, 'head'), may hold values from -0.09375 to 0.09375
- key_weight: bfloat16 [4096, 1024], P(None, 'head'), may hold values from -0.09375 to 0.09375
- value_weight: bfloat16 [4096, 1024], P(None, 'head'), may hold values from -0.09375 to 0.09375
- w_out: bfloat16 [4096, 4096], P('head'), may hold values from -0.09375 to 0.09375
Outputs:
- layer_out: bfloat16 [2048, 4096], P(('seq', 'head'))
Inputs may be any that keep to these rules, and one draw needn't show every extreme that they name: `block_order`: for each d, entries 2d and 2d+1 are two block numbers that sum to 15; every block number occurs once.
All inputs are finite; a program needn't handle non-finite values.
Results may differ from a plain program's by a relative error of at most 0.018.
The roundings to bfloat16 on the way count: a program that leaves them out, or rounds other values in their place, can miss the bound.
Values may be sent and summed in bfloat16 or wider, within the bound.
A program may use at most 64 MiB of HBM per device.

v0:
```python
import functools
import math

import jax
import jax.numpy as jnp
import numpy as np
from jax import lax
from jax.experimental import pallas as pl
from jax.experimental.pallas import tpu as pltpu
from jax.sharding import PartitionSpec as P

HEAD_SIZE = 128
NEGATIVE_FILLER = -1e30
ROPE_BASE = 500000.0
DOCS = 4
CORES = 2
SUB = 2
EARLY = 2
MESH = pl.DeviceIdType.MESH
F32 = jnp.float32
BF16 = jnp.bfloat16


def rotated(t, cosine, sine):
    heads = t.shape[1] // HEAD_SIZE
    pieces = []
    for h in range(heads):
        one = t[:, h * HEAD_SIZE:(h + 1) * HEAD_SIZE]
        pieces.append(one * cosine + pltpu.roll(one, HEAD_SIZE // 2, 1) * sine)
    return pieces


def kernel(
    X, Z, Y, NC, NO,
    order, hidden, seg, freq, wq, wk, wv, wo_hbm, out,
    xg, wb, wo, acc, cos_t, sin_t, kv, att, pb, rb, sb, fb, *rest,
):
    far_side, near_side = rest[:6], rest[6:12]
    (w_sem, wo_sem, hs_sem, hp_sem, hl_sem, hr_sem,
     ks_sem, kr_sem, ps_sem, pr_sem, ys_sem, yr_sem) = rest[12:]
    r, D = hidden.shape
    R = xg.shape[0]
    G = R // Y
    Cq, Ck = wq.shape[1], wk.shape[1]
    half = R // 2
    q_heads, kv_heads = Cq // HEAD_SIZE, Ck // HEAD_SIZE
    group = q_heads // kv_heads
    KW, NW = D // NC, D // NO
    s_id, h_id = lax.axis_index("seq"), lax.axis_index("head")
    y, c = h_id // CORES, h_id % CORES
    z, x = s_id // X, s_id % X
    partner = y * CORES + (1 - c)

    def peer_y(j):
        return lax.rem(y + j, Y)

    def w_copy(which, k):
        src = (wq, wk, wv)[which]
        col = (0, Cq, Cq + Ck)[which]
        rows = pl.ds(k * KW, KW)
        return pltpu.make_async_copy(
            src.at[rows, :], wb.at[rows, pl.ds(col, src.shape[1])], w_sem.at[which, k]
        )

    def wo_copy(n):
        cols = pl.ds(n * NW, NW)
        return pltpu.make_async_copy(wo_hbm.at[:, cols], wo.at[:, cols], wo_sem.at[n])

    for k in range(NC):
        w_copy(1, k).start()
        w_copy(2, k).start()

    barrier = pltpu.get_barrier_semaphore()

    def greet(sq, hd):
        pl.semaphore_signal(barrier, inc=1, device_id=(sq, hd), device_id_type=MESH)

    greet(s_id, partner)
    for j in range(1, Y):
        greet(s_id, peer_y(j) * CORES + c)
    for k in range(1, X):
        greet(z * X + lax.rem(x + k, X), h_id)

    @pl.when(z > 0)
    def _():
        greet(s_id - X, h_id)

    @pl.when(z < Z - 1)
    def _():
        greet(s_id + X, h_id)

    near = jnp.where(z > 0, 1, 0) + jnp.where(z < Z - 1, 1, 0)
    pl.semaphore_wait(barrier, 1 + (Y - 1) + (X - 1) + near)

    def hid_copy(origin, k, target, sem, from_input):
        cols = pl.ds(k * KW, KW)
        rows = pl.ds(origin * r, r)
        src = hidden.at[:, cols] if from_input else xg.at[rows, cols]
        return pltpu.make_async_remote_copy(
            src_ref=src, dst_ref=xg.at[rows, cols], send_sem=sem, recv_sem=hr_sem.at[origin, k],
            device_id=(s_id, target), device_id_type=MESH,
        )

    def hid_send(j, k):
        return hid_copy(h_id, k, peer_y(j) * CORES + c, hs_sem.at[j, k], True)

    def hid_pair(k):
        return hid_copy(h_id, k, partner, hp_sem.at[k], True)

    def hid_relay(j, k):
        return hid_copy(peer_y(j) * CORES + c, k, partner, hl_sem.at[j, k], False)

    def hid_from(origin, k):
        return hid_copy(origin, k, partner, hp_sem.at[k], False)

    for k in range(NC):
        hid_pair(k).start()
        for j in range(1, Y):
            hid_send(j, k).start()

    xg[pl.ds(h_id * r, r), :] = hidden[...]

    lane = lax.broadcasted_iota(jnp.int32, (half, HEAD_SIZE), 1)
    row = lax.broadcasted_iota(jnp.int32, (half, HEAD_SIZE), 0)
    for i in range(2):
        base = order[2 * s_id + i]
        angle = (row + base * half).astype(F32) * freq[...]
        cos_t[pl.ds(i * half, half), :] = jnp.cos(angle)
        sn = jnp.sin(angle)
        sin_t[pl.ds(i * half, half), :] = jnp.where(lane < HEAD_SIZE // 2, -sn, sn)

    starts = [
        jnp.sum(jnp.sum((seg[...] < v).astype(jnp.int32), axis=0, keepdims=True), axis=1, keepdims=True)
        for v in range(1, DOCS)
    ]
    for side, places in ((far_side, range(1, Y)), (near_side, (0,))):
        info = side[5]
        for i, j in enumerate(places):
            first = peer_y(j) * G
            pos = lax.broadcasted_iota(jnp.int32, (1, G), 1) + (
                order[2 * s_id + first // half] * half + lax.rem(first, half)
            )
            start = jnp.zeros_like(pos)
            for begun in starts:
                start = jnp.where(begun <= pos, jnp.maximum(start, begun), start)
            wide = len(places) * G
            for gh in range(info.shape[1] // wide):
                lanes = slice(gh * wide + i * G, gh * wide + (i + 1) * G)
                info[0:1, lanes] = pos
                info[1:2, lanes] = start

    B = G // SUB

    def kv_copy(zb, xb, u, target, way):
        slot = zb * X + xb
        rows = pl.ds(u * B, B)
        return pltpu.make_async_remote_copy(
            src_ref=kv.at[slot, rows, :], dst_ref=kv.at[slot, rows, :],
            send_sem=ks_sem.at[zb, u, way], recv_sem=kr_sem.at[slot, u],
            device_id=(target, h_id), device_id_type=MESH,
        )

    def kv_out(zb, u, up, down, act):
        @pl.when(up & (z < Z - 1))
        def _():
            act(kv_copy(zb, x, u, s_id + X, 0))

        @pl.when(down & (z > 0))
        def _():
            act(kv_copy(zb, x, u, s_id - X, 1))

        for k in range(1, X):
            act(kv_copy(zb, x, u, z * X + lax.rem(x + k, X), 1 + k))

    def kv_wait(zb, xb, u):
        kv_copy(zb, xb, u, s_id, 0).wait_recv()

    start_it = lambda cp: cp.start()
    sent = lambda cp: cp.wait_send()

    def forward(d, g):
        for e in range(SUB):
            u = g * SUB + e

            @pl.when((d < Z) & (z - d >= 0))
            def _():
                kv_wait(z - d, x, u)
                kv_out(z - d, u, True, False, start_it)

            @pl.when((d < Z) & (z + d < Z))
            def _():
                kv_wait(z + d, x, u)
                kv_out(z + d, u, False, True, start_it)

    def store_kv(g):
        rows = pl.ds(g * G, G)
        pieces = rotated(acc[:, Cq:Cq + Ck], cos_t[rows, :], sin_t[rows, :])
        for h in range(kv_heads):
            kv[s_id, rows, h * HEAD_SIZE:(h + 1) * HEAD_SIZE] = pieces[h].astype(BF16)
        kv[s_id, rows, Ck:2 * Ck] = acc[:, Cq + Ck:].astype(BF16)
        for e in range(SUB):
            kv_out(z, g * SUB + e, True, True, start_it)

    def store_q(g, side, place):
        rows = pl.ds(g * G, G)
        q = side[0]
        wide = q.shape[1] // group
        pieces = rotated(acc[:, :Cq], cos_t[rows, :], sin_t[rows, :])
        for h in range(q_heads):
            lo = (h % group) * wide + place * G
            q[h // group, lo:lo + G, :] = pieces[h].astype(BF16)

    def add_dot(g, k, lo, hi):
        span = pl.ds(k * KW, KW)
        acc[:, lo:hi] += jnp.dot(
            xg[pl.ds(g * G, G), span], wb[span, lo:hi], preferred_element_type=F32
        )

    acc[...] = jnp.zeros_like(acc)

    def first_kv(k, _):
        hid_from(partner, k).wait_recv()
        w_copy(1, k).wait()
        w_copy(2, k).wait()
        w_copy(0, k).start()
        add_dot(y, k, Cq, Cq + 2 * Ck)
        return 0

    lax.fori_loop(0, NC, first_kv, 0)
    store_kv(y)

    def first_q(k, _):
        w_copy(0, k).wait()
        wo_copy(k).start()
        add_dot(y, k, 0, Cq)
        return 0

    lax.fori_loop(0, NC, first_q, 0)
    store_q(y, near_side, 0)

    for j in range(1, Y):
        g = peer_y(j)
        acc[...] = jnp.zeros_like(acc)

        def arrive(k, _, j=j, g=g):
            @pl.when(k < NC)
            def _():
                hid_from(g * CORES + c, k).wait_recv()
                hid_relay(j, k).start()

            @pl.when(k > 0)
            def _():
                hid_from(g * CORES + (1 - c), k - 1).wait_recv()
                add_dot(g, k - 1, 0, Cq + 2 * Ck)

            if j == 1:
                @pl.when(k == NC // 2)
                def _():
                    forward(1, y)

                @pl.when(k == NC)
                def _():
                    forward(2, y)

            return 0

        lax.fori_loop(0, NC + 1, arrive, 0)
        store_kv(g)
        store_q(g, far_side, j - 1)

    for side in (far_side, near_side):
        side[1][...] = jnp.full_like(side[1], NEGATIVE_FILLER)
        side[2][...] = jnp.zeros_like(side[2])
        side[3][...] = jnp.zeros_like(side[3])
    scale = math.log2(math.e) / math.sqrt(HEAD_SIZE)
    nt = (((1,), (1,)), ((), ()))

    def attend(slot, side):
        q, m_s, l_s, o_s, bias, info = side
        chunk = bias.shape[1]
        krow = lax.broadcasted_iota(jnp.int32, (half, chunk), 0)
        for i in range(2):
            kpos = krow + order[2 * slot + i] * half
            ok = (kpos <= info[0:1, :]) & (kpos >= info[1:2, :])
            bias[i * half:(i + 1) * half, :] = jnp.where(ok, 0.0, NEGATIVE_FILLER)
        work = [(kh, w) for kh in range(kv_heads) for w in range(q.shape[1] // chunk)]
        span = lambda w: slice(w * chunk, (w + 1) * chunk)
        keys = [kv[slot, :, kh * HEAD_SIZE:(kh + 1) * HEAD_SIZE] for kh in range(kv_heads)]
        vals = [
            kv[slot, :, Ck + kh * HEAD_SIZE:Ck + (kh + 1) * HEAD_SIZE].T for kh in range(kv_heads)
        ]

        def scores(item):
            kh, w = item
            return lax.dot_general(keys[kh], q[kh, span(w), :], nt, preferred_element_type=F32)

        ahead = scores(work[0])
        for i, (kh, w) in enumerate(work):
            raw = ahead
            if i + 1 < len(work):
                ahead = scores(work[i + 1])
            cols = span(w)
            s = raw * scale + bias[...]
            old = m_s[kh:kh + 1, cols]
            new = jnp.maximum(old, jnp.max(s, axis=0, keepdims=True))
            p = jnp.exp2(s - new)
            alpha = jnp.exp2(old - new)
            m_s[kh:kh + 1, cols] = new
            l_s[kh:kh + 1, cols] = l_s[kh:kh + 1, cols] * alpha + jnp.sum(p, axis=0, keepdims=True)
            o_s[kh, :, cols] = o_s[kh, :, cols] * alpha + jnp.dot(
                vals[kh], p.astype(BF16), preferred_element_type=F32
            )

    def settle(side, lo):
        q, m_s, l_s, o_s, bias, info = side
        wide = q.shape[1] // group
        for h in range(q_heads):
            kh, gh = h // group, h % group
            lanes = slice(gh * wide, (gh + 1) * wide)
            att[lo:lo + wide, h * HEAD_SIZE:(h + 1) * HEAD_SIZE] = (
                o_s[kh, :, lanes] / l_s[kh:kh + 1, lanes]
            ).T.astype(BF16)

    def early(dist, xb):
        return (xb == x) & (dist <= EARLY)

    def stage(d, _):
        @pl.when(d >= 1)
        def _():
            for j in range(1, Y):
                forward(d, peer_y(j))

        def visit(i, _):
            side, k = i // X, lax.rem(i, X)
            dist = jnp.where(k == 0, d, d - 1)
            zb = jnp.where(side == 0, z - dist, z + dist)
            xb = lax.rem(x + k, X)
            ok = (zb >= 0) & (zb < Z) & (dist >= 0) & ((dist > 0) | (side == 0))

            @pl.when(ok)
            def _():
                @pl.when(k > 0)
                def _():
                    for u in range(Y * SUB):
                        kv_wait(zb, xb, u)

                attend(zb * X + xb, far_side)

                @pl.when(early(dist, xb))
                def _():
                    attend(zb * X + xb, near_side)

            return 0

        lax.fori_loop(0, 2 * X, visit, 0)
        forward(d + 3, y)
        return 0

    lax.fori_loop(0, Z + 1, stage, 0)
    settle(far_side, 0)

    def pair_copy(j, n):
        cols = pl.ds(n * NW, NW)
        return pltpu.make_async_remote_copy(
            src_ref=pb.at[j, 1 - c, :, cols], dst_ref=rb.at[j, :, cols],
            send_sem=ps_sem.at[j, n], recv_sem=pr_sem.at[j, n],
            device_id=(s_id, partner), device_id_type=MESH,
        )

    def far_copy(j, n):
        cols = pl.ds(n * NW, NW)
        return pltpu.make_async_remote_copy(
            src_ref=sb.at[j, :, cols], dst_ref=fb.at[j, :, cols],
            send_sem=ys_sem.at[j, n], recv_sem=yr_sem.at[j, n],
            device_id=(s_id, peer_y(j + 1) * CORES + c), device_id_type=MESH,
        )

    def pair_sum(j, n):
        cols = pl.ds(n * NW, NW)
        pair_copy(j, n).wait_recv()
        return pb[j, c, :, cols].astype(F32) + rb[j, :, cols].astype(F32)

    def project(i, _):
        @pl.when(i != (Y - 1) * NO)
        def _():
            ahead = jnp.where(i < (Y - 1) * NO, i, i - 1)
            j, n = ahead // NO, lax.rem(ahead, NO)
            cols = pl.ds(n * NW, NW)

            @pl.when(j == 0)
            def _():
                wo_copy(n).wait()

            part = jnp.dot(
                att[pl.ds(j * G, G), :], wo[:, cols], preferred_element_type=F32
            ).astype(BF16)
            for e in range(CORES):
                pb[j, e, :, cols] = part[e * r:(e + 1) * r, :]
            pair_copy(j, n).start()

        @pl.when((i > 0) & (i <= (Y - 1) * NO))
        def _():
            j, n = (i - 1) // NO, lax.rem(i - 1, NO)
            sb[j, :, pl.ds(n * NW, NW)] = pair_sum(j, n).astype(BF16)
            far_copy(j, n).start()

        return 0

    lax.fori_loop(0, (Y - 1) * NO + 1, project, 0)

    def rest_of(slot, _):
        zb, xb = slot // X, lax.rem(slot, X)
        dist = jnp.maximum(z - zb, zb - z)

        @pl.when(jnp.logical_not(early(dist, xb)))
        def _():
            attend(slot, near_side)

        return 0

    lax.fori_loop(0, Z * X, rest_of, 0)
    settle(near_side, (Y - 1) * G)
    lax.fori_loop((Y - 1) * NO + 1, Y * NO + 1, project, 0)

    def finish(n, _):
        total = pair_sum(Y - 1, n)
        for j in range(Y - 1):
            far_copy(j, n).wait_recv()
            total = total + fb[j, :, pl.ds(n * NW, NW)].astype(F32)
        out[:, pl.ds(n * NW, NW)] = total.astype(BF16)
        return 0

    lax.fori_loop(0, NO, finish, 0)

    def drain_hidden(k, _):
        hid_pair(k).wait_send()
        for j in range(1, Y):
            hid_send(j, k).wait_send()
            hid_relay(j, k).wait_send()
        return 0

    lax.fori_loop(0, NC, drain_hidden, 0)

    def drain_kv(zb, _):
        for u in range(Y * SUB):
            kv_out(zb, u, zb <= z, zb >= z, sent)
        return 0

    lax.fori_loop(0, Z, drain_kv, 0)

    def drain_out(n, _):
        for j in range(Y):
            pair_copy(j, n).wait_send()
        for j in range(Y - 1):
            far_copy(j, n).wait_send()
        return 0

    lax.fori_loop(0, NO, drain_out, 0)


def on_device(X, Z, Y, hidden, block_order, segment_ids, w_query, key_weight, value_weight, w_out):
    r, D = hidden.shape
    S, H = X * Z, Y * CORES
    R = r * H
    G = R // Y
    Cq, Ck = w_query.shape[1], key_weight.shape[1]
    W = Cq + 2 * Ck
    q_heads = Cq // HEAD_SIZE
    NC = NO = max(1, D // 512)
    exponent = np.arange(HEAD_SIZE // 2, dtype=np.float64) * 2.0 / HEAD_SIZE
    freqs = np.tile(ROPE_BASE ** (-exponent), 2).astype(np.float32)[None, :]
    dma = pltpu.SemaphoreType.DMA
    kv_heads = Ck // HEAD_SIZE
    group = q_heads // kv_heads

    def half_scratch(rows):
        together = 2 if rows % HEAD_SIZE == 0 and group % 2 == 0 else group
        lanes = group * rows
        return [
            pltpu.VMEM((kv_heads, lanes, HEAD_SIZE), BF16),
            pltpu.VMEM((kv_heads, lanes), F32),
            pltpu.VMEM((kv_heads, lanes), F32),
            pltpu.VMEM((kv_heads, HEAD_SIZE, lanes), F32),
            pltpu.VMEM((R, together * rows), F32),
            pltpu.VMEM((2, together * rows), jnp.int32),
        ]

    far = max(1, Y - 1)
    vmem = pl.BlockSpec(memory_space=pltpu.VMEM)
    anywhere = pl.BlockSpec(memory_space=pl.ANY)
    return pl.pallas_call(
        functools.partial(kernel, X, Z, Y, NC, NO),
        out_shape=jax.ShapeDtypeStruct((r, D), BF16),
        in_specs=[pl.BlockSpec(memory_space=pltpu.SMEM), vmem, vmem, vmem] + [anywhere] * 4,
        out_specs=vmem,
        scratch_shapes=[
            pltpu.VMEM((R, D), BF16),
            pltpu.VMEM((D, W), BF16),
            pltpu.VMEM((Cq, D), BF16),
            pltpu.VMEM((G, W), F32),
            pltpu.VMEM((R, HEAD_SIZE), F32),
            pltpu.VMEM((R, HEAD_SIZE), F32),
            pltpu.VMEM((S, R, 2 * Ck), BF16),
            pltpu.VMEM((R, Cq), BF16),
            pltpu.VMEM((Y, CORES, r, D), BF16),
            pltpu.VMEM((Y, r, D), BF16),
            pltpu.VMEM((far, r, D), BF16),
            pltpu.VMEM((far, r, D), BF16),
            *half_scratch((Y - 1) * G),
            *half_scratch(G),
            dma((3, NC)), dma((NO,)),
            dma((Y, NC)), dma((NC,)), dma((Y, NC)), dma((H, NC)),
            dma((Z, Y * SUB, 1 + X)), dma((S, Y * SUB)),
            dma((Y, NO)), dma((Y, NO)), dma((far, NO)), dma((far, NO)),
        ],
        compiler_params=pltpu.CompilerParams(
            collective_id=0, has_side_effects=True, vmem_limit_bytes=60 * 1024 * 1024
        ),
    )(
        block_order, hidden, segment_ids.reshape(block_order.shape[0], -1), jnp.asarray(freqs),
        w_query, key_weight, value_weight, w_out,
    )


def solution(mesh):
    seq, head = mesh.shape["seq"], mesh.shape["head"]
    X = 1
    while 4 * X * X <= seq and seq % (2 * X) == 0:
        X *= 2
    placed = (
        P(("seq", "head"), None),
        P(),
        P(),
        P(None, "head"),
        P(None, "head"),
        P(None, "head"),
        P("head", None),
    )
    return jax.shard_map(
        functools.partial(on_device, X, seq // X, head // CORES),
        mesh=mesh, in_specs=placed, out_specs=P(("seq", "head"), None), check_vma=False,
    )
```

profile of v0, /device:TPU:0, one launch (start us, length us, event | category | flops | bytes accessed | tf_op | source)
XLA Modules:
  0.0 58.5 jit_solution(3155784902245853020)
XLA Ops:
  0.0 56.7 %shard_map.82 = bf16[64,4096]{1,0:T(8,128)(2,1)} custom-call(s32[16]{0:T(128)} %order.1, bf16[64,4096]{1,0:T(8,128)(2,1)} %hidden.1, s32[16,128]{1,0:T(8,128)} %bitcast.1, f32[1,128]{1,0:T(1,128)} %constant.2.clone.freq, bf16[4096,1024]{1,0:T(8,128)(2,1)} %wq.1, bf16[4096,256]{1,0:T(8,128)(2,1)} %wk.1, bf16[4096,256]{1,0:T(8,128)(2,1)} %wv.1, ...), custom_call_target="tpu_custom_call" | custom-call | tf_op jit(solution)/shard_map/pallas_call | solution.py:491
  56.7 1.9 %copy.10 = bf16[64,4096]{1,0:T(8,128)(2,1)} copy(bf16[64,4096]{1,0:T(8,128)(2,1)} %shard_map.82) | data formatting | bytes 1048576
where the time goes:
time: 58.7 us; the launch traced here: 58.5 us
  Pallas kernels  56.7 us (97%)
  local copies, waits for them, and re-layouts  1.87 us (3%)
    pallas_call x1, Pallas kernels, on_device(): pl.pallas_call(functools.partial(kernel, X, Z, Y, NC, NO), out_shape=jax....  56.7 us
    unnamed x1, local copies, waits for them, and re-layouts  1.87 us

commit v1 on v0

v1 whole, which is shorter than its diff:
```python
import functools
import math

import jax
import jax.numpy as jnp
import numpy as np
from jax import lax
from jax.experimental import pallas as pl
from jax.experimental.pallas import tpu as pltpu
from jax.sharding import PartitionSpec as P

HEAD_SIZE = 128
NEGATIVE_FILLER = -1e30
ROPE_BASE = 500000.0
DOCS = 4
CORES = 2
LAG = 3
MESH = pl.DeviceIdType.MESH
F32 = jnp.float32
BF16 = jnp.bfloat16


def rotated(t, cosine, sine):
    heads = t.shape[1] // HEAD_SIZE
    pieces = []
    for h in range(heads):
        one = t[:, h * HEAD_SIZE:(h + 1) * HEAD_SIZE]
        pieces.append(one * cosine + pltpu.roll(one, HEAD_SIZE // 2, 1) * sine)
    return pieces


def kernel(
    X, Z, Y, NO, NP,
    order, hidden, seg_hbm, freq_hbm, wq, wk, wv, wo_hbm, out,
    seg, freq, xg, wb, wo, acc, cos_t, sin_t, kv, att, keep, give, rb, sb, fb, *rest,
):
    far_side, near_side = rest[:6], rest[6:12]
    (in_sem, hn_sem, wkv_sem, wq_sem, wo_sem, hs_sem, hp_sem, hd_sem, hr_sem,
     xs_sem, zs_sem, kc_sem, kx_sem, ps_sem, pf_sem, pn_sem, ys_sem, yr_sem) = rest[12:]
    r, D = hidden.shape
    R = xg.shape[0]
    Cq, Ck = wq.shape[1], wk.shape[1]
    half = R // 2
    q_heads, kv_heads = Cq // HEAD_SIZE, Ck // HEAD_SIZE
    group = q_heads // kv_heads
    W = Cq + 2 * Ck
    near_rows, far_rows = CORES * r, R - CORES * r
    part = r // 2
    s_id, h_id = lax.axis_index("seq"), lax.axis_index("head")
    y, c = h_id // CORES, h_id % CORES
    z, x = s_id // X, s_id % X
    partner = y * CORES + (1 - c)

    def peer_y(j):
        return lax.rem(y + j, Y)

    def far_at(j, e):
        return near_rows + e * (Y - 1) * r + (j - 1) * r

    runs = [(0, r, h_id * r), (r, r, partner * r)]
    for e in range(2):
        for j in range(1, Y):
            for i, core in enumerate((c, 1 - c)):
                runs.append((far_at(j, e) + i * part, part, (peer_y(j) * CORES + core) * r + e * part))
    pieces = [(0, r), (r, r), (near_rows, (Y - 1) * r), (near_rows + (Y - 1) * r, (Y - 1) * r)]
    units = [(0, near_rows), (near_rows, far_rows)]

    def place(slot, first):
        return order[2 * slot + first // half] * half + lax.rem(first, half)

    barrier = pltpu.get_barrier_semaphore()

    def greet(sq, hd):
        pl.semaphore_signal(barrier, inc=1, device_id=(sq, hd), device_id_type=MESH)

    greet(s_id, partner)
    for j in range(1, Y):
        greet(s_id, peer_y(j) * CORES + c)
    for k in range(1, X):
        greet(z * X + lax.rem(x + k, X), h_id)

    for d in range(1, Z):
        greet(lax.rem(z + d, Z) * X + x, h_id)

    own_rows = pltpu.make_async_copy(hidden, xg.at[pl.ds(0, r), :], hn_sem)
    own_rows.start()
    seg_copy = pltpu.make_async_copy(seg_hbm, seg, in_sem.at[0])
    freq_copy = pltpu.make_async_copy(freq_hbm, freq, in_sem.at[1])
    freq_copy.start()
    seg_copy.start()
    wk_copy = pltpu.make_async_copy(wk, wb.at[:, pl.ds(Cq, Ck)], wkv_sem.at[0])
    wv_copy = pltpu.make_async_copy(wv, wb.at[:, pl.ds(Cq + Ck, Ck)], wkv_sem.at[1])
    wq_copy = pltpu.make_async_copy(wq, wb.at[:, pl.ds(0, Cq)], wq_sem)
    wo_copy = pltpu.make_async_copy(wo_hbm, wo, wo_sem)
    wk_copy.start()
    wv_copy.start()

    pl.semaphore_wait(barrier, 1 + (Y - 1) + (X - 1) + (Z - 1))

    def hid_pair():
        return pltpu.make_async_remote_copy(
            src_ref=xg.at[pl.ds(0, r), :], dst_ref=xg.at[pl.ds(r, r), :],
            send_sem=hs_sem, recv_sem=hp_sem,
            device_id=(s_id, partner), device_id_type=MESH,
        )

    def hid_send(j, e):
        return pltpu.make_async_remote_copy(
            src_ref=xg.at[pl.ds(e * part, part), :], dst_ref=xg.at[pl.ds(far_at(Y - j, e), part), :],
            send_sem=hs_sem, recv_sem=hd_sem.at[Y - j - 1, e],
            device_id=(s_id, peer_y(j) * CORES + c), device_id_type=MESH,
        )

    def hid_direct(j, e):
        rows = xg.at[pl.ds(far_at(j, e), part), :]
        return pltpu.make_async_remote_copy(
            src_ref=rows, dst_ref=rows, send_sem=hs_sem, recv_sem=hd_sem.at[j - 1, e],
            device_id=(s_id, partner), device_id_type=MESH,
        )

    def hid_relay(j, e):
        return pltpu.make_async_remote_copy(
            src_ref=xg.at[pl.ds(far_at(j, e), part), :],
            dst_ref=xg.at[pl.ds(far_at(j, e) + part, part), :],
            send_sem=hs_sem, recv_sem=hr_sem.at[j - 1, e],
            device_id=(s_id, partner), device_id_type=MESH,
        )

    own_rows.wait()
    hid_pair().start()
    for e in range(2):
        for j in range(1, Y):
            hid_send(j, e).start()
    wq_copy.start()

    freq_copy.wait()
    for lo, n, first in runs:
        lane = lax.broadcasted_iota(jnp.int32, (n, HEAD_SIZE), 1)
        row = lax.broadcasted_iota(jnp.int32, (n, HEAD_SIZE), 0)
        angle = (row + place(s_id, first)).astype(F32) * freq[...]
        cos_t[lo:lo + n, :] = jnp.cos(angle)
        sn = jnp.sin(angle)
        sin_t[lo:lo + n, :] = jnp.where(lane < HEAD_SIZE // 2, -sn, sn)

    def kv_rows(zb, xb, lo, n):
        return kv.at[pl.ds((zb * X + xb) * R + lo, n), :]

    def col_copy(zb, p, target, sem):
        rows = kv_rows(zb, x, *pieces[p])
        return pltpu.make_async_remote_copy(
            src_ref=rows, dst_ref=rows, send_sem=sem, recv_sem=kc_sem.at[zb, p],
            device_id=(target, h_id), device_id_type=MESH,
        )

    def cross_copy(zb, xb, p, way, target, sem):
        rows = kv_rows(zb, xb, *pieces[p])
        return pltpu.make_async_remote_copy(
            src_ref=rows, dst_ref=rows, send_sem=sem, recv_sem=kx_sem.at[way - 1, zb, p],
            device_id=(target, h_id), device_id_type=MESH,
        )

    def send_x(zb, p):
        for k in range(1, X):
            cross_copy(zb, x, p, X - k, z * X + lax.rem(x + k, X), xs_sem).start()

    def send_up(zb, p):
        @pl.when(z < Z - 1)
        def _():
            col_copy(zb, p, s_id + X, zs_sem).start()

    def send_down(zb, p):
        @pl.when(z > 0)
        def _():
            col_copy(zb, p, s_id - X, zs_sem).start()

    def send_own(p):
        if p < 2:
            send_up(z, p)
            send_down(z, p)
        else:
            for d in range(Z - 1, 0, -1):
                @pl.when(z + d < Z)
                def _(d=d):
                    col_copy(z, p, s_id + d * X, zs_sem).start()

                @pl.when(z - d >= 0)
                def _(d=d):
                    col_copy(z, p, s_id - d * X, zs_sem).start()
        send_x(z, p)

    def pass_on(d, p):
        @pl.when(z - d >= 0)
        def _():
            col_copy(z - d, p, s_id, zs_sem).wait_recv()
            if p < 2:
                send_up(z - d, p)
            if d > 1 or p < 2:
                send_x(z - d, p)

        @pl.when(z + d < Z)
        def _():
            col_copy(z + d, p, s_id, zs_sem).wait_recv()
            if p < 2:
                send_down(z + d, p)
            if d > 1 or p < 2:
                send_x(z + d, p)

    def cross_wait(zb, way, p):
        cross_copy(zb, lax.rem(x + way, X), p, way, s_id, xs_sem).wait_recv()

    def cross_on(way, p):
        xb = lax.rem(x + way, X)
        cross_wait(z, way, p)

        @pl.when(z < Z - 1)
        def _():
            cross_copy(z, xb, p, way, s_id + X, zs_sem).start()

        @pl.when(z > 0)
        def _():
            cross_copy(z, xb, p, way, s_id - X, zs_sem).start()

    def store_kv(p):
        lo, n = pieces[p]
        got = jnp.dot(xg[lo:lo + n, :], wb[:, Cq:W], preferred_element_type=F32)
        turned = rotated(got[:, :Ck], cos_t[lo:lo + n, :], sin_t[lo:lo + n, :])
        rows = pl.ds(s_id * R + lo, n)
        for h in range(kv_heads):
            kv[rows, h * HEAD_SIZE:(h + 1) * HEAD_SIZE] = turned[h].astype(BF16)
        kv[rows, Ck:2 * Ck] = got[:, Ck:].astype(BF16)
        send_own(p)

    def store_q(u, side):
        lo, n = units[u]
        q = side[0]
        acc[0:n, :] = jnp.dot(xg[lo:lo + n, :], wb[:, :Cq], preferred_element_type=F32)
        turned = rotated(acc[0:n, :], cos_t[lo:lo + n, :], sin_t[lo:lo + n, :])
        for h in range(q_heads):
            at = (h % group) * n
            q[h // group, at:at + n, :] = turned[h].astype(BF16)

    wk_copy.wait()
    wv_copy.wait()
    store_kv(0)

    seg_copy.wait()
    starts = [
        jnp.sum(jnp.sum((seg[...] < v).astype(jnp.int32), axis=0, keepdims=True), axis=1, keepdims=True)
        for v in range(1, DOCS)
    ]
    for u, side in enumerate((near_side, far_side)):
        lo, n = units[u]
        info = side[5]
        for at, m, first in runs:
            if not lo <= at < lo + n:
                continue
            pos = lax.broadcasted_iota(jnp.int32, (1, m), 1) + place(s_id, first)
            start = jnp.zeros_like(pos)
            for begun in starts:
                start = jnp.where(begun <= pos, jnp.maximum(start, begun), start)
            for gh in range(info.shape[1] // n):
                lanes = slice(gh * n + at - lo, gh * n + at - lo + m)
                info[0:1, lanes] = pos
                info[1:2, lanes] = start
    for side in (far_side, near_side):
        side[1][...] = jnp.full_like(side[1], NEGATIVE_FILLER)
        side[2][...] = jnp.zeros_like(side[2])
        side[3][...] = jnp.zeros_like(side[3])

    hid_pair().wait_recv()
    store_kv(1)
    wo_copy.start()
    wq_copy.wait()
    store_q(0, near_side)

    scale = math.log2(math.e) / math.sqrt(HEAD_SIZE)
    nt = (((1,), (1,)), ((), ()))

    def attend(slot, u, side):
        q, m_s, l_s, o_s, bias, info = side
        chunk = bias.shape[1]
        lo, n = units[u]
        for at, m, first in runs:
            if not lo <= at < lo + n:
                continue
            kpos = lax.broadcasted_iota(jnp.int32, (m, chunk), 0) + place(slot, first)
            ok = (kpos <= info[0:1, :]) & (kpos >= info[1:2, :])
            bias[at - lo:at - lo + m, :] = jnp.where(ok, 0.0, NEGATIVE_FILLER)
        work = [(kh, w) for kh in range(kv_heads) for w in range(q.shape[1] // chunk)]
        span = lambda w: slice(w * chunk, (w + 1) * chunk)
        rows = pl.ds(slot * R + lo, n)
        keys = [kv[rows, kh * HEAD_SIZE:(kh + 1) * HEAD_SIZE] for kh in range(kv_heads)]
        vals = [
            kv[rows, Ck + kh * HEAD_SIZE:Ck + (kh + 1) * HEAD_SIZE].T for kh in range(kv_heads)
        ]

        def scores(item):
            kh, w = item
            return lax.dot_general(keys[kh], q[kh, span(w), :], nt, preferred_element_type=F32)

        ahead = scores(work[0])
        for i, (kh, w) in enumerate(work):
            raw = ahead
            if i + 1 < len(work):
                ahead = scores(work[i + 1])
            cols = span(w)
            s = raw * scale + bias[0:n, :]
            old = m_s[kh:kh + 1, cols]
            new = jnp.maximum(old, jnp.max(s, axis=0, keepdims=True))
            p = jnp.exp2(s - new)
            alpha = jnp.exp2(old - new)
            m_s[kh:kh + 1, cols] = new
            l_s[kh:kh + 1, cols] = l_s[kh:kh + 1, cols] * alpha + jnp.sum(p, axis=0, keepdims=True)
            o_s[kh, :, cols] = o_s[kh, :, cols] * alpha + jnp.dot(
                vals[kh], p.astype(BF16), preferred_element_type=F32
            )

    def visit(u, side, first, last, ways, wait):
        A, B = ways

        def one(i, _):
            d, rest_i = i // (2 * (B - A)), lax.rem(i, 2 * (B - A))
            sign, way = rest_i // (B - A), A + lax.rem(rest_i, B - A)
            zb = jnp.where(sign == 0, z - d, z + d)

            @pl.when((zb >= 0) & (zb < Z) & ((d > 0) | (sign == 0)))
            def _():
                if wait:
                    for p in wait:
                        cross_wait(zb, way, p)
                attend(zb * X + lax.rem(x + way, X), u, side)

            return 0

        lax.fori_loop(first * 2 * (B - A), last * 2 * (B - A), one, 0)

    def settle(side, lo):
        q, m_s, l_s, o_s, bias, info = side
        wide = q.shape[1] // group
        for h in range(q_heads):
            kh, gh = h // group, h % group
            lanes = slice(gh * wide, (gh + 1) * wide)
            att[lo:lo + wide, h * HEAD_SIZE:(h + 1) * HEAD_SIZE] = (
                o_s[kh, :, lanes] / l_s[kh:kh + 1, lanes]
            ).T.astype(BF16)

    column, others = (0, 1), (1, X)


    def relay(first, last, p):
        for d in range(first, min(last, Z)):
            pass_on(d, p)

    def hidden_on(e):
        for j in range(1, Y):
            hid_direct(j, e).wait_recv()
            hid_relay(j, e).start()

    def hidden_in(e):
        for j in range(1, Y):
            hid_relay(j, e).wait_recv()

    N_BOTH, F_BOTH = (0, 1), (2, 3)

    relay(1, 2, 0)
    visit(0, near_side, 0, 1, column, ())
    relay(1, 2, 1)
    visit(0, near_side, 1, min(2, Z), column, ())
    hidden_on(0)
    hidden_in(0)
    store_kv(2)
    relay(2, 3, 0)
    relay(2, 3, 1)
    visit(0, near_side, 0, 1, others, N_BOTH)
    visit(0, near_side, 2, min(3, Z), column, ())
    visit(0, near_side, 1, min(2, Z), others, N_BOTH)
    hidden_on(1)
    hidden_in(1)
    store_kv(3)
    for way in range(1, X):
        cross_on(way, 2)
    store_q(1, far_side)
    relay(3, Z, 0)
    relay(3, Z, 1)
    visit(0, far_side, 0, min(2, Z), (0, X), ())
    relay(1, Z, 2)
    for way in range(1, X):
        cross_on(way, 3)
    visit(0, far_side, 2, Z, column, ())
    relay(1, Z, 3)
    visit(0, far_side, 2, Z, others, N_BOTH)
    visit(1, far_side, 0, Z, column, ())
    visit(1, far_side, 0, 1, others, ())
    visit(1, far_side, 1, Z, others, F_BOTH)
    settle(far_side, near_rows)
    wo_copy.wait()

    NW, PW = D // NO, D // NP

    def pair_far(j, n):
        cols = pl.ds(n * NW, NW)
        return pltpu.make_async_remote_copy(
            src_ref=give.at[j, :, cols], dst_ref=rb.at[j, :, cols],
            send_sem=ps_sem, recv_sem=pf_sem.at[j - 1, n],
            device_id=(s_id, partner), device_id_type=MESH,
        )

    def pair_near(n):
        cols = pl.ds(n * PW, PW)
        return pltpu.make_async_remote_copy(
            src_ref=give.at[0, :, cols], dst_ref=rb.at[0, :, cols],
            send_sem=ps_sem, recv_sem=pn_sem.at[n],
            device_id=(s_id, partner), device_id_type=MESH,
        )

    def far_copy(j, n):
        cols = pl.ds(n * NW, NW)
        return pltpu.make_async_remote_copy(
            src_ref=sb.at[j - 1, :, cols], dst_ref=fb.at[j - 1, :, cols],
            send_sem=ys_sem, recv_sem=yr_sem.at[j - 1, n],
            device_id=(s_id, peer_y(j) * CORES + c), device_id_type=MESH,
        )

    def project_far(n, _):
        @pl.when(n < NO)
        def _():
            cols = pl.ds(n * NW, NW)
            got = jnp.dot(att[near_rows:R, :], wo[:, cols], preferred_element_type=F32).astype(BF16)
            for j in range(1, Y):
                for e in range(2):
                    at = far_at(j, e) - near_rows
                    keep[j, e * part:(e + 1) * part, cols] = got[at:at + part, :]
                    give[j, e * part:(e + 1) * part, cols] = got[at + part:at + r, :]
                pair_far(j, n).start()

        @pl.when(n >= LAG)
        def _():
            cols = pl.ds((n - LAG) * NW, NW)
            for j in range(1, Y):
                pair_far(j, n - LAG).wait_recv()
                sb[j - 1, :, cols] = (keep[j, :, cols].astype(F32) + rb[j, :, cols].astype(F32)).astype(BF16)
                far_copy(j, n - LAG).start()

        return 0

    lax.fori_loop(0, NO + LAG, project_far, 0)
    visit(0, near_side, 3, Z, column, ())
    visit(0, near_side, 2, Z, others, ())
    visit(1, near_side, 0, Z, (0, X), ())
    settle(near_side, 0)

    def project_near(n, _):
        cols = pl.ds(n * PW, PW)
        got = jnp.dot(att[0:near_rows, :], wo[:, cols], preferred_element_type=F32).astype(BF16)
        keep[0, :, cols] = got[:r, :]
        give[0, :, cols] = got[r:, :]
        pair_near(n).start()
        return 0

    lax.fori_loop(0, NP, project_near, 0)

    for n in range(NP):
        pair_near(n).wait_recv()

    def finish(n, _):
        cols = pl.ds(n * NW, NW)
        total = keep[0, :, cols].astype(F32) + rb[0, :, cols].astype(F32)
        for j in range(1, Y):
            far_copy(j, n).wait_recv()
            total = total + fb[j - 1, :, cols].astype(F32)
        out[:, cols] = total.astype(BF16)
        return 0

    lax.fori_loop(0, NO, finish, 0)

    def drain(ref, sem):
        pltpu.make_async_copy(ref, ref, sem).wait()

    drain(xg.at[pl.ds(0, (2 * Y - 1) * r), :], hs_sem)
    drain(give, ps_sem)
    drain(sb, ys_sem)
    for zz in range(Z):
        ups, downs = (zz + 1 if zz < Z - 1 else 0), (Z - zz if zz > 0 else 0)
        beside = (zz > 0) + (zz < Z - 1)
        along = (ups + downs) * near_rows + (Z - 1 + (X - 1) * beside) * far_rows
        over = (X - 1) * (Z * R - beside * far_rows)

        @pl.when(z == zz)
        def _(along=along, over=over):
            drain(kv.at[pl.ds(0, along), :], zs_sem)
            drain(kv.at[pl.ds(0, over), :], xs_sem)


def on_device(X, Z, Y, hidden, block_order, segment_ids, w_query, key_weight, value_weight, w_out):
    r, D = hidden.shape
    S, H = X * Z, Y * CORES
    R = r * H
    Cq, Ck = w_query.shape[1], key_weight.shape[1]
    W = Cq + 2 * Ck
    q_heads = Cq // HEAD_SIZE
    NO, NP = max(1, D // 512), max(1, D // 1024)
    exponent = np.arange(HEAD_SIZE // 2, dtype=np.float64) * 2.0 / HEAD_SIZE
    freqs = np.tile(ROPE_BASE ** (-exponent), 2).astype(np.float32)[None, :]
    dma = pltpu.SemaphoreType.DMA
    kv_heads = Ck // HEAD_SIZE
    group = q_heads // kv_heads
    near_rows, far_rows = CORES * r, R - CORES * r
    segments = segment_ids.reshape(block_order.shape[0], -1)

    def half_scratch(rows):
        together = 2 if rows % HEAD_SIZE == 0 and group % 2 == 0 else group
        lanes = group * rows
        return [
            pltpu.VMEM((kv_heads, lanes, HEAD_SIZE), BF16),
            pltpu.VMEM((kv_heads, lanes), F32),
            pltpu.VMEM((kv_heads, lanes), F32),
            pltpu.VMEM((kv_heads, HEAD_SIZE, lanes), F32),
            pltpu.VMEM((max(near_rows, far_rows), together * rows), F32),
            pltpu.VMEM((2, together * rows), jnp.int32),
        ]

    far = max(1, Y - 1)
    anywhere = pl.BlockSpec(memory_space=pl.ANY)
    return pl.pallas_call(
        functools.partial(kernel, X, Z, Y, NO, NP),
        out_shape=pltpu.VMEM((r, D), BF16),
        in_specs=[pl.BlockSpec(memory_space=pltpu.SMEM)] + [anywhere] * 7,
        out_specs=pl.BlockSpec(memory_space=pltpu.VMEM),
        scratch_shapes=[
            pltpu.VMEM(segments.shape, jnp.int32),
            pltpu.VMEM((1, HEAD_SIZE), F32),
            pltpu.VMEM((R, D), BF16),
            pltpu.VMEM((D, W), BF16),
            pltpu.VMEM((Cq, D), BF16),
            pltpu.VMEM((max(near_rows, far_rows), Cq), F32),
            pltpu.VMEM((R, HEAD_SIZE), F32),
            pltpu.VMEM((R, HEAD_SIZE), F32),
            pltpu.VMEM((S * R, 2 * Ck), BF16),
            pltpu.VMEM((R, Cq), BF16),
            pltpu.VMEM((Y, r, D), BF16),
            pltpu.VMEM((Y, r, D), BF16),
            pltpu.VMEM((Y, r, D), BF16),
            pltpu.VMEM((far, r, D), BF16),
            pltpu.VMEM((far, r, D), BF16),
            *half_scratch(far_rows),
            *half_scratch(near_rows),
            dma((2,)), dma, dma((2,)), dma, dma,
            dma, dma, dma((far, 2)), dma((far, 2)),
            dma, dma, dma((Z, 4)), dma((max(1, X - 1), Z, 4)),
            dma, dma((far, NO)), dma((NP,)), dma, dma((far, NO)),
        ],
        compiler_params=pltpu.CompilerParams(
            collective_id=0, has_side_effects=True, vmem_limit_bytes=60 * 1024 * 1024
        ),
    )(
        block_order, hidden, segments, jnp.asarray(freqs),
        w_query, key_weight, value_weight, w_out,
    )


def solution(mesh):
    seq, head = mesh.shape["seq"], mesh.shape["head"]
    X = 1
    while 4 * X * X <= seq and seq % (2 * X) == 0:
        X *= 2
    placed = (
        P(("seq", "head"), None),
        P(),
        P(),
        P(None, "head"),
        P(None, "head"),
        P(None, "head"),
        P("head", None),
    )
    return jax.shard_map(
        functools.partial(on_device, X, seq // X, head // CORES),
        mesh=mesh, in_specs=placed, out_specs=P(("seq", "head"), None), check_vma=False,
    )
```

time: 58.7 us -> 53.3 us (0.908)
  Pallas kernels: 56.7 us -> 52.4 us
  local copies, waits for them, and re-layouts: 1.87 us -> 0.8 us
    pallas_call x1, Pallas kernels: 56.7 us -> 52.4 us  [on_device(): pl.pallas_call(functools.partial(kernel, X, Z, Y, NO, NP), out_shape=pltp...]
    unnamed x1, local copies, waits for them, and re-layouts: 1.87 us -> 0.8 us
where the time goes in v1:
time: 53.3 us; the launch traced here: 53.2 us
  Pallas kernels  52.4 us (98%)
  local copies, waits for them, and re-layouts  0.8 us (2%)
    pallas_call x1, Pallas kernels, on_device(): pl.pallas_call(functools.partial(kernel, X, Z, Y, NO, NP), out_shape=pltp...  52.4 us

profile of v1, /device:TPU:0, one launch (start us, length us, event | category | flops | bytes accessed | tf_op | source)
XLA Modules:
  0.0 53.2 jit_solution(6733526845794310044)
XLA Ops:
  0.0 52.4 %shard_map.82 = bf16[64,4096]{1,0:T(8,128)(2,1)S(1)} custom-call(s32[16]{0:T(128)} %order.1, bf16[64,4096]{1,0:T(8,128)(2,1)} %hidden.1, s32[16,128]{1,0:T(8,128)} %bitcast.1, f32[1,128]{1,0:T(1,128)} %constant.2.clone.freq_hbm, bf16[4096,1024]{1,0:T(8,128)(2,1)} %wq.1, bf16[4096,256]{1,0:T(8,128)(2,1)} %wk.1, bf16[4096,256]{1,0:T(8,128)(2,1)} %wv.1, ...), custom_call_target="tpu_custom_call" | custom-call | tf_op jit(solution)/shard_map/pallas_call | solution.py:524
  52.4 0.8 %copy.10 = bf16[64,4096]{1,0:T(8,128)(2,1)} copy(bf16[64,4096]{1,0:T(8,128)(2,1)S(1)} %shard_map.82) | data formatting | bytes 1048576

commit v2 on v1

--- a/solution.py
+++ b/solution.py
@@ -79,8 +79,13 @@
     for k in range(1, X):
         greet(z * X + lax.rem(x + k, X), h_id)
 
-    for d in range(1, Z):
-        greet(lax.rem(z + d, Z) * X + x, h_id)
+    @pl.when(z > 0)
+    def _():
+        greet(s_id - X, h_id)
+
+    @pl.when(z < Z - 1)
+    def _():
+        greet(s_id + X, h_id)
 
     own_rows = pltpu.make_async_copy(hidden, xg.at[pl.ds(0, r), :], hn_sem)
     own_rows.start()
@@ -95,7 +100,8 @@
     wk_copy.start()
     wv_copy.start()
 
-    pl.semaphore_wait(barrier, 1 + (Y - 1) + (X - 1) + (Z - 1))
+    near = jnp.where(z > 0, 1, 0) + jnp.where(z < Z - 1, 1, 0)
+    pl.semaphore_wait(barrier, 1 + (Y - 1) + (X - 1) + near)
 
     def hid_pair():
         return pltpu.make_async_remote_copy(
@@ -173,19 +179,21 @@
         def _():
             col_copy(zb, p, s_id - X, zs_sem).start()
 
+    def send_along(p, d):
+        @pl.when(z + d < Z)
+        def _():
+            col_copy(z, p, s_id + d * X, zs_sem).start()
+
+        @pl.when(z - d >= 0)
+        def _():
+            col_copy(z, p, s_id - d * X, zs_sem).start()
+
+    def send_far(p):
+        for d in range(2, Z):
+            send_along(p, d)
+
     def send_own(p):
-        if p < 2:
-            send_up(z, p)
-            send_down(z, p)
-        else:
-            for d in range(Z - 1, 0, -1):
-                @pl.when(z + d < Z)
-                def _(d=d):
-                    col_copy(z, p, s_id + d * X, zs_sem).start()
-
-                @pl.when(z - d >= 0)
-                def _(d=d):
-                    col_copy(z, p, s_id - d * X, zs_sem).start()
+        send_along(p, 1)
         send_x(z, p)
 
     def pass_on(d, p):
@@ -369,28 +377,33 @@
     hidden_on(0)
     hidden_in(0)
     store_kv(2)
-    relay(2, 3, 0)
-    relay(2, 3, 1)
+    relay(2, Z - 1, 0)
+    relay(2, Z - 1, 1)
+    send_far(2)
     visit(0, near_side, 0, 1, others, N_BOTH)
-    visit(0, near_side, 2, min(3, Z), column, ())
+    visit(0, near_side, 2, Z - 1, column, ())
     visit(0, near_side, 1, min(2, Z), others, N_BOTH)
     hidden_on(1)
     hidden_in(1)
     store_kv(3)
+    send_far(3)
     for way in range(1, X):
         cross_on(way, 2)
     store_q(1, far_side)
-    relay(3, Z, 0)
-    relay(3, Z, 1)
     visit(0, far_side, 0, min(2, Z), (0, X), ())
     relay(1, Z, 2)
     for way in range(1, X):
         cross_on(way, 3)
-    visit(0, far_side, 2, Z, column, ())
+    visit(0, far_side, 2, Z - 1, column, ())
+    visit(0, far_side, 2, Z - 1, others, N_BOTH)
     relay(1, Z, 3)
-    visit(0, far_side, 2, Z, others, N_BOTH)
-    visit(1, far_side, 0, Z, column, ())
+    relay(Z - 1, Z, 0)
+    relay(Z - 1, Z, 1)
+    visit(1, far_side, 0, 1, column, ())
     visit(1, far_side, 0, 1, others, ())
+    visit(1, far_side, 1, Z, column, ())
+    visit(0, far_side, Z - 1, Z, column, ())
+    visit(0, far_side, Z - 1, Z, others, N_BOTH)
     visit(1, far_side, 1, Z, others, F_BOTH)
     settle(far_side, near_rows)
     wo_copy.wait()

time: 53.3 us -> 55.6 us (1.043)
  Pallas kernels: 52.4 us -> 54.6 us
    pallas_call x1, Pallas kernels: 52.4 us -> 54.6 us  [on_device(): pl.pallas_call(functools.partial(kernel, X, Z, Y, NO, NP), out_shape=pltp...]
where the time goes in v2:
time: 55.6 us; the launch traced here: 55.4 us
  Pallas kernels  54.6 us (98%)
  local copies, waits for them, and re-layouts  0.8 us (1%)
    pallas_call x1, Pallas kernels, on_device(): pl.pallas_call(functools.partial(kernel, X, Z, Y, NO, NP), out_shape=pltp...  54.6 us

profile of v2, /device:TPU:0, one launch (start us, length us, event | category | flops | bytes accessed | tf_op | source)
XLA Modules:
  0.0 55.4 jit_solution(1094043405023477581)
XLA Ops:
  0.0 54.6 %shard_map.82 = bf16[64,4096]{1,0:T(8,128)(2,1)S(1)} custom-call(s32[16]{0:T(128)} %order.1, bf16[64,4096]{1,0:T(8,128)(2,1)} %hidden.1, s32[16,128]{1,0:T(8,128)} %bitcast.1, f32[1,128]{1,0:T(1,128)} %constant.2.clone.freq_hbm, bf16[4096,1024]{1,0:T(8,128)(2,1)} %wq.1, bf16[4096,256]{1,0:T(8,128)(2,1)} %wk.1, bf16[4096,256]{1,0:T(8,128)(2,1)} %wv.1, ...), custom_call_target="tpu_custom_call" | custom-call | tf_op jit(solution)/shard_map/pallas_call | solution.py:537
  54.6 0.8 %copy.10 = bf16[64,4096]{1,0:T(8,128)(2,1)} copy(bf16[64,4096]{1,0:T(8,128)(2,1)S(1)} %shard_map.82) | data formatting | bytes 1048576

commit v3 on v2

--- a/solution.py
+++ b/solution.py
@@ -15,6 +15,7 @@
 DOCS = 4
 CORES = 2
 LAG = 3
+AHEAD = 2
 MESH = pl.DeviceIdType.MESH
 F32 = jnp.float32
 BF16 = jnp.bfloat16
@@ -30,13 +31,13 @@
 
 
 def kernel(
-    X, Z, Y, NO, NP,
+    X, Z, Y, PARTS, NO, NP,
     order, hidden, seg_hbm, freq_hbm, wq, wk, wv, wo_hbm, out,
     seg, freq, xg, wb, wo, acc, cos_t, sin_t, kv, att, keep, give, rb, sb, fb, *rest,
 ):
     far_side, near_side = rest[:6], rest[6:12]
     (in_sem, hn_sem, wkv_sem, wq_sem, wo_sem, hs_sem, hp_sem, hd_sem, hr_sem,
-     xs_sem, zs_sem, kc_sem, kx_sem, ps_sem, pf_sem, pn_sem, ys_sem, yr_sem) = rest[12:]
+     xs_sem, zs_sem, kc_sem, kx_sem, ps_sem, pf_sem, pn_sem, ys_sem, yr_sem, ready) = rest[12:]
     r, D = hidden.shape
     R = xg.shape[0]
     Cq, Ck = wq.shape[1], wk.shape[1]
@@ -45,7 +46,10 @@
     group = q_heads // kv_heads
     W = Cq + 2 * Ck
     near_rows, far_rows = CORES * r, R - CORES * r
-    part = r // 2
+    part = r // PARTS
+    wide_part = (Y - 1) * CORES * part
+    S = X * Z
+    TOGETHER = math.gcd(S, 4)
     s_id, h_id = lax.axis_index("seq"), lax.axis_index("head")
     y, c = h_id // CORES, h_id % CORES
     z, x = s_id // X, s_id % X
@@ -55,14 +59,14 @@
         return lax.rem(y + j, Y)
 
     def far_at(j, e):
-        return near_rows + e * (Y - 1) * r + (j - 1) * r
+        return near_rows + e * wide_part + (j - 1) * CORES * part
 
     runs = [(0, r, h_id * r), (r, r, partner * r)]
-    for e in range(2):
+    for e in range(PARTS):
         for j in range(1, Y):
             for i, core in enumerate((c, 1 - c)):
                 runs.append((far_at(j, e) + i * part, part, (peer_y(j) * CORES + core) * r + e * part))
-    pieces = [(0, r), (r, r), (near_rows, (Y - 1) * r), (near_rows + (Y - 1) * r, (Y - 1) * r)]
+    pieces = [(0, r), (r, r)] + [(near_rows + e * wide_part, wide_part) for e in range(PARTS)]
     units = [(0, near_rows), (near_rows, far_rows)]
 
     def place(slot, first):
@@ -103,6 +107,25 @@
     near = jnp.where(z > 0, 1, 0) + jnp.where(z < Z - 1, 1, 0)
     pl.semaphore_wait(barrier, 1 + (Y - 1) + (X - 1) + near)
 
+    def tell(side, ok):
+        @pl.when(ok)
+        def _():
+            pl.semaphore_signal(
+                ready.at[side], inc=1, device_id=(s_id + (X if side == 0 else -X), h_id),
+                device_id_type=MESH,
+            )
+
+    def hear(d):
+        for side, there in ((0, z - d >= 0), (1, z + d < Z)):
+            @pl.when(there)
+            def _(side=side):
+                pl.semaphore_wait(ready.at[side], 1)
+
+            tell(side, there & ((z < Z - 1) if side == 0 else (z > 0)))
+
+    tell(0, (z > 0) & (z < Z - 1))
+    tell(1, (z < Z - 1) & (z > 0))
+
     def hid_pair():
         return pltpu.make_async_remote_copy(
             src_ref=xg.at[pl.ds(0, r), :], dst_ref=xg.at[pl.ds(r, r), :],
@@ -134,7 +157,7 @@
 
     own_rows.wait()
     hid_pair().start()
-    for e in range(2):
+    for e in range(PARTS):
         for j in range(1, Y):
             hid_send(j, e).start()
     wq_copy.start()
@@ -188,30 +211,27 @@
         def _():
             col_copy(z, p, s_id - d * X, zs_sem).start()
 
-    def send_far(p):
-        for d in range(2, Z):
+    def send_own(p):
+        for d in range(1 if p < 2 else Z - 1, 0, -1):
             send_along(p, d)
-
-    def send_own(p):
-        send_along(p, 1)
         send_x(z, p)
 
+    def at_end(a, b):
+        return (a == 0) | (a == Z - 1) | (b == 0) | (b == Z - 1)
+
     def pass_on(d, p):
-        @pl.when(z - d >= 0)
-        def _():
-            col_copy(z - d, p, s_id, zs_sem).wait_recv()
-            if p < 2:
-                send_up(z - d, p)
-            if d > 1 or p < 2:
-                send_x(z - d, p)
-
-        @pl.when(z + d < Z)
-        def _():
-            col_copy(z + d, p, s_id, zs_sem).wait_recv()
-            if p < 2:
-                send_down(z + d, p)
-            if d > 1 or p < 2:
-                send_x(z + d, p)
+        for side, zb, there in ((0, z - d, z - d >= 0), (1, z + d, z + d < Z)):
+            @pl.when(there)
+            def _(side=side, zb=zb):
+                col_copy(zb, p, s_id, zs_sem).wait_recv()
+                if p < 2 and d == 1:
+                    (send_up if side == 0 else send_down)(zb, p)
+                if p < 2 or d > 1:
+                    send_x(zb, p)
+                else:
+                    @pl.when(jnp.logical_not(at_end(z, zb)))
+                    def _():
+                        send_x(zb, p)
 
     def cross_wait(zb, way, p):
         cross_copy(zb, lax.rem(x + way, X), p, way, s_id, xs_sem).wait_recv()
@@ -220,11 +240,11 @@
         xb = lax.rem(x + way, X)
         cross_wait(z, way, p)
 
-        @pl.when(z < Z - 1)
+        @pl.when((z < Z - 1) & at_end(z, z + 1))
         def _():
             cross_copy(z, xb, p, way, s_id + X, zs_sem).start()
 
-        @pl.when(z > 0)
+        @pl.when((z > 0) & at_end(z, z - 1))
         def _():
             cross_copy(z, xb, p, way, s_id - X, zs_sem).start()
 
@@ -277,6 +297,8 @@
 
     hid_pair().wait_recv()
     store_kv(1)
+    for d in range(2, min(3, Z)):
+        hear(d)
     wo_copy.start()
     wq_copy.wait()
     store_q(0, near_side)
@@ -284,35 +306,45 @@
     scale = math.log2(math.e) / math.sqrt(HEAD_SIZE)
     nt = (((1,), (1,)), ((), ()))
 
-    def attend(slot, u, side):
+    def nearest(n):
+        low = jnp.minimum(z, Z - 1 - z)
+        d = (n + 1) // 2
+        both = jnp.where(lax.rem(n, 2) == 1, z - d, z + d)
+        return jnp.where(n <= 2 * low, both, jnp.where(z < Z - 1 - z, n, Z - 1 - n))
+
+    def attend(slots, u, side):
         q, m_s, l_s, o_s, bias, info = side
         chunk = bias.shape[1]
         lo, n = units[u]
-        for at, m, first in runs:
-            if not lo <= at < lo + n:
-                continue
-            kpos = lax.broadcasted_iota(jnp.int32, (m, chunk), 0) + place(slot, first)
-            ok = (kpos <= info[0:1, :]) & (kpos >= info[1:2, :])
-            bias[at - lo:at - lo + m, :] = jnp.where(ok, 0.0, NEGATIVE_FILLER)
+        total = len(slots) * n
+        for t, slot in enumerate(slots):
+            for at, m, first in runs:
+                if not lo <= at < lo + n:
+                    continue
+                kpos = lax.broadcasted_iota(jnp.int32, (m, chunk), 0) + place(slot, first)
+                ok = (kpos <= info[0:1, :]) & (kpos >= info[1:2, :])
+                bias[t * n + at - lo:t * n + at - lo + m, :] = jnp.where(ok, 0.0, NEGATIVE_FILLER)
         work = [(kh, w) for kh in range(kv_heads) for w in range(q.shape[1] // chunk)]
         span = lambda w: slice(w * chunk, (w + 1) * chunk)
-        rows = pl.ds(slot * R + lo, n)
-        keys = [kv[rows, kh * HEAD_SIZE:(kh + 1) * HEAD_SIZE] for kh in range(kv_heads)]
-        vals = [
-            kv[rows, Ck + kh * HEAD_SIZE:Ck + (kh + 1) * HEAD_SIZE].T for kh in range(kv_heads)
-        ]
+
+        def gathered(col):
+            cols = slice(col, col + HEAD_SIZE)
+            return jnp.concatenate([kv[pl.ds(slot * R + lo, n), cols] for slot in slots], axis=0)
+
+        keys = [gathered(kh * HEAD_SIZE) for kh in range(kv_heads)]
+        vals = [gathered(Ck + kh * HEAD_SIZE).T for kh in range(kv_heads)]
 
         def scores(item):
             kh, w = item
             return lax.dot_general(keys[kh], q[kh, span(w), :], nt, preferred_element_type=F32)
 
-        ahead = scores(work[0])
+        ahead = [scores(item) for item in work[:AHEAD]]
         for i, (kh, w) in enumerate(work):
-            raw = ahead
-            if i + 1 < len(work):
-                ahead = scores(work[i + 1])
+            raw = ahead.pop(0)
+            if i + AHEAD < len(work):
+                ahead.append(scores(work[i + AHEAD]))
             cols = span(w)
-            s = raw * scale + bias[0:n, :]
+            s = raw * scale + bias[0:total, :]
             old = m_s[kh:kh + 1, cols]
             new = jnp.maximum(old, jnp.max(s, axis=0, keepdims=True))
             p = jnp.exp2(s - new)
@@ -323,24 +355,16 @@
                 vals[kh], p.astype(BF16), preferred_element_type=F32
             )
 
-    def visit(u, side, first, last, ways, wait):
-        A, B = ways
-
+    def visit(u, side, first, last):
         def one(i, _):
-            d, rest_i = i // (2 * (B - A)), lax.rem(i, 2 * (B - A))
-            sign, way = rest_i // (B - A), A + lax.rem(rest_i, B - A)
-            zb = jnp.where(sign == 0, z - d, z + d)
-
-            @pl.when((zb >= 0) & (zb < Z) & ((d > 0) | (sign == 0)))
-            def _():
-                if wait:
-                    for p in wait:
-                        cross_wait(zb, way, p)
-                attend(zb * X + lax.rem(x + way, X), u, side)
-
+            slots = []
+            for t in range(TOGETHER):
+                i_t = i * TOGETHER + t
+                slots.append(nearest(i_t // X) * X + lax.rem(x + lax.rem(i_t, X), X))
+            attend(slots, u, side)
             return 0
 
-        lax.fori_loop(first * 2 * (B - A), last * 2 * (B - A), one, 0)
+        lax.fori_loop(first // TOGETHER, last // TOGETHER, one, 0)
 
     def settle(side, lo):
         q, m_s, l_s, o_s, bias, info = side
@@ -368,43 +392,49 @@
         for j in range(1, Y):
             hid_relay(j, e).wait_recv()
 
-    N_BOTH, F_BOTH = (0, 1), (2, 3)
-
+    def crossed(first, last, parts):
+        for n in range(first, last):
+            for way in range(1, X):
+                for p in parts:
+                    cross_wait(nearest(jnp.int32(n)), way, p)
+
+    N_ALL, F_ALL = (0, 1), tuple(range(2, 2 + PARTS))
+    last = PARTS - 1
+
+    for d in range(3, Z):
+        hear(d)
+        send_along(0, d)
+        send_along(1, d)
     relay(1, 2, 0)
-    visit(0, near_side, 0, 1, column, ())
     relay(1, 2, 1)
-    visit(0, near_side, 1, min(2, Z), column, ())
-    hidden_on(0)
-    hidden_in(0)
-    store_kv(2)
-    relay(2, Z - 1, 0)
-    relay(2, Z - 1, 1)
-    send_far(2)
-    visit(0, near_side, 0, 1, others, N_BOTH)
-    visit(0, near_side, 2, Z - 1, column, ())
-    visit(0, near_side, 1, min(2, Z), others, N_BOTH)
-    hidden_on(1)
-    hidden_in(1)
-    store_kv(3)
-    send_far(3)
+    for e in range(PARTS):
+        if e == last:
+            relay(2, 3, 0)
+            relay(3, Z, 0)
+            relay(3, Z, 1)
+            relay(2, 3, 1)
+        hidden_on(e)
+        hidden_in(e)
+        store_kv(2 + e)
+    for p in F_ALL[:-1]:
+        for way in range(1, X):
+            cross_on(way, p)
+    store_q(1, far_side)
+    crossed(0, 2, N_ALL)
+    visit(0, far_side, 0, S // 2)
+    for p in F_ALL[:-1]:
+        for d in range(Z - 1, 0, -1):
+            relay(d, d + 1, p)
     for way in range(1, X):
-        cross_on(way, 2)
-    store_q(1, far_side)
-    visit(0, far_side, 0, min(2, Z), (0, X), ())
-    relay(1, Z, 2)
-    for way in range(1, X):
-        cross_on(way, 3)
-    visit(0, far_side, 2, Z - 1, column, ())
-    visit(0, far_side, 2, Z - 1, others, N_BOTH)
-    relay(1, Z, 3)
-    relay(Z - 1, Z, 0)
-    relay(Z - 1, Z, 1)
-    visit(1, far_side, 0, 1, column, ())
-    visit(1, far_side, 0, 1, others, ())
-    visit(1, far_side, 1, Z, column, ())
-    visit(0, far_side, Z - 1, Z, column, ())
-    visit(0, far_side, Z - 1, Z, others, N_BOTH)
-    visit(1, far_side, 1, Z, others, F_BOTH)
+        cross_on(way, 1 + PARTS)
+    for d in range(Z - 1, 0, -1):
+        relay(d, d + 1, 1 + PARTS)
+    crossed(2, Z, N_ALL)
+    visit(0, far_side, S // 2, S)
+    crossed(1, 2, F_ALL)
+    visit(1, far_side, 0, S // 2)
+    crossed(2, Z, F_ALL)
+    visit(1, far_side, S // 2, S)
     settle(far_side, near_rows)
     wo_copy.wait()
 
@@ -440,10 +470,10 @@
             cols = pl.ds(n * NW, NW)
             got = jnp.dot(att[near_rows:R, :], wo[:, cols], preferred_element_type=F32).astype(BF16)
             for j in range(1, Y):
-                for e in range(2):
+                for e in range(PARTS):
                     at = far_at(j, e) - near_rows
                     keep[j, e * part:(e + 1) * part, cols] = got[at:at + part, :]
-                    give[j, e * part:(e + 1) * part, cols] = got[at + part:at + r, :]
+                    give[j, e * part:(e + 1) * part, cols] = got[at + part:at + 2 * part, :]
                 pair_far(j, n).start()
 
         @pl.when(n >= LAG)
@@ -457,9 +487,8 @@
         return 0
 
     lax.fori_loop(0, NO + LAG, project_far, 0)
-    visit(0, near_side, 3, Z, column, ())
-    visit(0, near_side, 2, Z, others, ())
-    visit(1, near_side, 0, Z, (0, X), ())
+    visit(0, near_side, 0, S)
+    visit(1, near_side, 0, S)
     settle(near_side, 0)
 
     def project_near(n, _):
@@ -493,10 +522,12 @@
     drain(give, ps_sem)
     drain(sb, ys_sem)
     for zz in range(Z):
-        ups, downs = (zz + 1 if zz < Z - 1 else 0), (Z - zz if zz > 0 else 0)
-        beside = (zz > 0) + (zz < Z - 1)
-        along = (ups + downs) * near_rows + (Z - 1 + (X - 1) * beside) * far_rows
-        over = (X - 1) * (Z * R - beside * far_rows)
+        ends = (0, Z - 1)
+        beside = [zb for zb in (zz - 1, zz + 1) if 0 <= zb < Z]
+        bent = sum(zz in ends or zb in ends for zb in beside)
+        early = len(beside) + 2 * (len(beside) == 2) + max(0, zz - 2) + max(0, Z - 3 - zz)
+        along = early * near_rows + (Z - 1 + (X - 1) * bent) * far_rows
+        over = (X - 1) * (Z * R - bent * far_rows)
 
         @pl.when(z == zz)
         def _(along=along, over=over):
@@ -512,6 +543,7 @@
     W = Cq + 2 * Ck
     q_heads = Cq // HEAD_SIZE
     NO, NP = max(1, D // 512), max(1, D // 1024)
+    PARTS = max(1, min(2, r // 16))
     exponent = np.arange(HEAD_SIZE // 2, dtype=np.float64) * 2.0 / HEAD_SIZE
     freqs = np.tile(ROPE_BASE ** (-exponent), 2).astype(np.float32)[None, :]
     dma = pltpu.SemaphoreType.DMA
@@ -521,21 +553,21 @@
     segments = segment_ids.reshape(block_order.shape[0], -1)
 
     def half_scratch(rows):
-        together = 2 if rows % HEAD_SIZE == 0 and group % 2 == 0 else group
+        together = 1 if rows % HEAD_SIZE == 0 else group
         lanes = group * rows
         return [
             pltpu.VMEM((kv_heads, lanes, HEAD_SIZE), BF16),
             pltpu.VMEM((kv_heads, lanes), F32),
             pltpu.VMEM((kv_heads, lanes), F32),
             pltpu.VMEM((kv_heads, HEAD_SIZE, lanes), F32),
-            pltpu.VMEM((max(near_rows, far_rows), together * rows), F32),
+            pltpu.VMEM((math.gcd(S, 4) * max(near_rows, far_rows), together * rows), F32),
             pltpu.VMEM((2, together * rows), jnp.int32),
         ]
 
     far = max(1, Y - 1)
     anywhere = pl.BlockSpec(memory_space=pl.ANY)
     return pl.pallas_call(
-        functools.partial(kernel, X, Z, Y, NO, NP),
+        functools.partial(kernel, X, Z, Y, PARTS, NO, NP),
         out_shape=pltpu.VMEM((r, D), BF16),
         in_specs=[pl.BlockSpec(memory_space=pltpu.SMEM)] + [anywhere] * 7,
         out_specs=pl.BlockSpec(memory_space=pltpu.VMEM),
@@ -558,9 +590,10 @@
             *half_scratch(far_rows),
             *half_scratch(near_rows),
             dma((2,)), dma, dma((2,)), dma, dma,
-            dma, dma, dma((far, 2)), dma((far, 2)),
-            dma, dma, dma((Z, 4)), dma((max(1, X - 1), Z, 4)),
+            dma, dma, dma((far, PARTS)), dma((far, PARTS)),
+            dma, dma, dma((Z, 2 + PARTS)), dma((max(1, X - 1), Z, 2 + PARTS)),
             dma, dma((far, NO)), dma((NP,)), dma, dma((far, NO)),
+            pltpu.SemaphoreType.REGULAR((2,)),
         ],
         compiler_params=pltpu.CompilerParams(
             collective_id=0, has_side_effects=True, vmem_limit_bytes=60 * 1024 * 1024

time: 55.6 us -> 49.9 us (0.90)
  Pallas kernels: 54.6 us -> 49 us
    pallas_call x1, Pallas kernels: 54.6 us -> 49 us  [on_device(): pl.pallas_call(functools.partial(kernel, X, Z, Y, PARTS, NO, NP), out_sha...]
where the time goes in v3:
time: 49.9 us; the launch traced here: 49.8 us
  Pallas kernels  49 us (98%)
  local copies, waits for them, and re-layouts  0.8 us (2%)
    pallas_call x1, Pallas kernels, on_device(): pl.pallas_call(functools.partial(kernel, X, Z, Y, PARTS, NO, NP), out_sha...  49 us

profile of v3, /device:TPU:0, one launch (start us, length us, event | category | flops | bytes accessed | tf_op | source)
XLA Modules:
  0.0 49.8 jit_solution(4014712325477256075)
XLA Ops:
  0.0 49.0 %shard_map.82 = bf16[64,4096]{1,0:T(8,128)(2,1)S(1)} custom-call(s32[16]{0:T(128)} %order.1, bf16[64,4096]{1,0:T(8,128)(2,1)} %hidden.1, s32[16,128]{1,0:T(8,128)} %bitcast.1, f32[1,128]{1,0:T(1,128)} %constant.2.clone.freq_hbm, bf16[4096,1024]{1,0:T(8,128)(2,1)} %wq.1, bf16[4096,256]{1,0:T(8,128)(2,1)} %wk.1, bf16[4096,256]{1,0:T(8,128)(2,1)} %wv.1, ...), custom_call_target="tpu_custom_call" | custom-call | tf_op jit(solution)/shard_map/pallas_call | solution.py:569
  49.0 0.8 %copy.10 = bf16[64,4096]{1,0:T(8,128)(2,1)} copy(bf16[64,4096]{1,0:T(8,128)(2,1)S(1)} %shard_map.82) | data formatting | bytes 1048576

commit v4 on v3

--- a/solution.py
+++ b/solution.py
@@ -32,8 +32,8 @@
 
 def kernel(
     X, Z, Y, PARTS, NO, NP,
-    order, hidden, seg_hbm, freq_hbm, wq, wk, wv, wo_hbm, out,
-    seg, freq, xg, wb, wo, acc, cos_t, sin_t, kv, att, keep, give, rb, sb, fb, *rest,
+    order_hbm, hidden, seg_hbm, freq_hbm, wq, wk, wv, wo_hbm, out,
+    order, seg, freq, xg, wb, wo, acc, cos_t, sin_t, kv, att, keep, give, rb, sb, fb, *rest,
 ):
     far_side, near_side = rest[:6], rest[6:12]
     (in_sem, hn_sem, wkv_sem, wq_sem, wo_sem, hs_sem, hp_sem, hd_sem, hr_sem,
@@ -95,7 +95,9 @@
     own_rows.start()
     seg_copy = pltpu.make_async_copy(seg_hbm, seg, in_sem.at[0])
     freq_copy = pltpu.make_async_copy(freq_hbm, freq, in_sem.at[1])
+    order_copy = pltpu.make_async_copy(order_hbm, order, in_sem.at[2])
     freq_copy.start()
+    order_copy.start()
     seg_copy.start()
     wk_copy = pltpu.make_async_copy(wk, wb.at[:, pl.ds(Cq, Ck)], wkv_sem.at[0])
     wv_copy = pltpu.make_async_copy(wv, wb.at[:, pl.ds(Cq + Ck, Ck)], wkv_sem.at[1])
@@ -163,6 +165,7 @@
     wq_copy.start()
 
     freq_copy.wait()
+    order_copy.wait()
     for lo, n, first in runs:
         lane = lax.broadcasted_iota(jnp.int32, (n, HEAD_SIZE), 1)
         row = lax.broadcasted_iota(jnp.int32, (n, HEAD_SIZE), 0)
@@ -224,7 +227,7 @@
             @pl.when(there)
             def _(side=side, zb=zb):
                 col_copy(zb, p, s_id, zs_sem).wait_recv()
-                if p < 2 and d == 1:
+                if p < 2:
                     (send_up if side == 0 else send_down)(zb, p)
                 if p < 2 or d > 1:
                     send_x(zb, p)
@@ -360,7 +363,7 @@
             slots = []
             for t in range(TOGETHER):
                 i_t = i * TOGETHER + t
-                slots.append(nearest(i_t // X) * X + lax.rem(x + lax.rem(i_t, X), X))
+                slots.append(nearest(lax.rem(i_t, Z)) * X + lax.rem(x + i_t // Z, X))
             attend(slots, u, side)
             return 0
 
@@ -403,15 +406,11 @@
 
     for d in range(3, Z):
         hear(d)
-        send_along(0, d)
-        send_along(1, d)
     relay(1, 2, 0)
     relay(1, 2, 1)
     for e in range(PARTS):
         if e == last:
             relay(2, 3, 0)
-            relay(3, Z, 0)
-            relay(3, Z, 1)
             relay(2, 3, 1)
         hidden_on(e)
         hidden_in(e)
@@ -419,22 +418,25 @@
     for p in F_ALL[:-1]:
         for way in range(1, X):
             cross_on(way, p)
+    for d in range(Z - 1, 1, -1):
+        for p in F_ALL[:-1]:
+            relay(d, d + 1, p)
     store_q(1, far_side)
-    crossed(0, 2, N_ALL)
-    visit(0, far_side, 0, S // 2)
     for p in F_ALL[:-1]:
-        for d in range(Z - 1, 0, -1):
-            relay(d, d + 1, p)
+        relay(1, 2, p)
+    relay(3, Z, 0)
+    relay(3, Z, 1)
+    for d in range(Z - 1, 1, -1):
+        relay(d, d + 1, 1 + PARTS)
     for way in range(1, X):
         cross_on(way, 1 + PARTS)
-    for d in range(Z - 1, 0, -1):
-        relay(d, d + 1, 1 + PARTS)
-    crossed(2, Z, N_ALL)
-    visit(0, far_side, S // 2, S)
-    crossed(1, 2, F_ALL)
-    visit(1, far_side, 0, S // 2)
-    crossed(2, Z, F_ALL)
-    visit(1, far_side, S // 2, S)
+    relay(1, 2, 1 + PARTS)
+    visit(0, far_side, 0, Z)
+    visit(1, far_side, 0, Z)
+    crossed(0, Z, N_ALL)
+    visit(0, far_side, Z, S)
+    crossed(1, Z, F_ALL)
+    visit(1, far_side, Z, S)
     settle(far_side, near_rows)
     wo_copy.wait()
 
@@ -525,7 +527,7 @@
         ends = (0, Z - 1)
         beside = [zb for zb in (zz - 1, zz + 1) if 0 <= zb < Z]
         bent = sum(zz in ends or zb in ends for zb in beside)
-        early = len(beside) + 2 * (len(beside) == 2) + max(0, zz - 2) + max(0, Z - 3 - zz)
+        early = (zz + 1) * (zz < Z - 1) + (Z - zz) * (zz > 0)
         along = early * near_rows + (Z - 1 + (X - 1) * bent) * far_rows
         over = (X - 1) * (Z * R - bent * far_rows)
 
@@ -569,9 +571,10 @@
     return pl.pallas_call(
         functools.partial(kernel, X, Z, Y, PARTS, NO, NP),
         out_shape=pltpu.VMEM((r, D), BF16),
-        in_specs=[pl.BlockSpec(memory_space=pltpu.SMEM)] + [anywhere] * 7,
+        in_specs=[anywhere] * 8,
         out_specs=pl.BlockSpec(memory_space=pltpu.VMEM),
         scratch_shapes=[
+            pltpu.SMEM(block_order.shape, jnp.int32),
             pltpu.VMEM(segments.shape, jnp.int32),
             pltpu.VMEM((1, HEAD_SIZE), F32),
             pltpu.VMEM((R, D), BF16),
@@ -589,7 +592,7 @@
             pltpu.VMEM((far, r, D), BF16),
             *half_scratch(far_rows),
             *half_scratch(near_rows),
-            dma((2,)), dma, dma((2,)), dma, dma,
+            dma((3,)), dma, dma((2,)), dma, dma,
             dma, dma, dma((far, PARTS)), dma((far, PARTS)),
             dma, dma, dma((Z, 2 + PARTS)), dma((max(1, X - 1), Z, 2 + PARTS)),
             dma, dma((far, NO)), dma((NP,)), dma, dma((far, NO)),

time: 49.9 us -> 47.8 us (0.958)
  Pallas kernels: 49 us -> 46.8 us
    pallas_call x1, Pallas kernels: 49 us -> 46.8 us  [on_device(): pl.pallas_call(functools.partial(kernel, X, Z, Y, PARTS, NO, NP), out_sha...]
where the time goes in v4:
time: 47.8 us; the launch traced here: 47.6 us
  Pallas kernels  46.8 us (98%)
  local copies, waits for them, and re-layouts  0.8 us (2%)
    pallas_call x1, Pallas kernels, on_device(): pl.pallas_call(functools.partial(kernel, X, Z, Y, PARTS, NO, NP), out_sha...  46.8 us

profile of v4, /device:TPU:0, one launch (start us, length us, event | category | flops | bytes accessed | tf_op | source)
XLA Modules:
  0.0 47.6 jit_solution(11217967192499644545)
XLA Ops:
  0.0 46.8 %shard_map.82 = bf16[64,4096]{1,0:T(8,128)(2,1)S(1)} custom-call(s32[16]{0:T(128)} %order_hbm.1, bf16[64,4096]{1,0:T(8,128)(2,1)} %hidden.1, s32[16,128]{1,0:T(8,128)} %bitcast.1, f32[1,128]{1,0:T(1,128)} %constant.2.clone.freq_hbm, bf16[4096,1024]{1,0:T(8,128)(2,1)} %wq.1, bf16[4096,256]{1,0:T(8,128)(2,1)} %wk.1, bf16[4096,256]{1,0:T(8,128)(2,1)} %wv.1, ...), custom_call_target="tpu_custom_call" | custom-call | tf_op jit(solution)/shard_map/pallas_call | solution.py:571
  46.8 0.8 %copy.10 = bf16[64,4096]{1,0:T(8,128)(2,1)} copy(bf16[64,4096]{1,0:T(8,128)(2,1)S(1)} %shard_map.82) | data formatting | bytes 1048576

commit v5 on v4

--- a/solution.py
+++ b/solution.py
@@ -369,6 +369,13 @@
 
         lax.fori_loop(first // TOGETHER, last // TOGETHER, one, 0)
 
+    def visit_these(u, side, pairs, count=TOGETHER):
+        for first in range(0, len(pairs), count):
+            attend(
+                [nearest(jnp.int32(n)) * X + lax.rem(x + way, X) for n, way in pairs[first:first + count]],
+                u, side,
+            )
+
     def settle(side, lo):
         q, m_s, l_s, o_s, bias, info = side
         wide = q.shape[1] // group
@@ -422,6 +429,11 @@
         for p in F_ALL[:-1]:
             relay(d, d + 1, p)
     store_q(1, far_side)
+    soon = [(n, 0) for n in range(min(3, Z))] + [(0, way) for way in range(1, X)]
+    soon = soon[:len(soon) // TOGETHER * TOGETHER]
+    later = [(n, way) for n in range(Z) for way in range(X) if (n, way) not in soon]
+    crossed(0, 1, N_ALL)
+    visit_these(0, far_side, soon)
     for p in F_ALL[:-1]:
         relay(1, 2, p)
     relay(3, Z, 0)
@@ -431,12 +443,15 @@
     for way in range(1, X):
         cross_on(way, 1 + PARTS)
     relay(1, 2, 1 + PARTS)
-    visit(0, far_side, 0, Z)
-    visit(1, far_side, 0, Z)
-    crossed(0, Z, N_ALL)
-    visit(0, far_side, Z, S)
-    crossed(1, Z, F_ALL)
-    visit(1, far_side, Z, S)
+    visit_these(1, far_side, [(n, 0) for n in range(Z)])
+    crossed(1, Z, N_ALL)
+    visit_these(0, far_side, later)
+    half_far = [(n, way) for way in range(1, X) for n in (0, Z - 1)]
+    rest_far = [(n, way) for way in range(1, X) for n in range(1, Z - 1)]
+    crossed(Z - 1, Z, F_ALL)
+    visit_these(1, far_side, half_far, max(1, TOGETHER // 2))
+    crossed(1, Z - 1, F_ALL)
+    visit_these(1, far_side, rest_far, max(1, TOGETHER // 2))
     settle(far_side, near_rows)
     wo_copy.wait()
 
@@ -454,7 +469,7 @@
         cols = pl.ds(n * PW, PW)
         return pltpu.make_async_remote_copy(
             src_ref=give.at[0, :, cols], dst_ref=rb.at[0, :, cols],
-            send_sem=ps_sem, recv_sem=pn_sem.at[n],
+            send_sem=ps_sem, recv_sem=pn_sem,
             device_id=(s_id, partner), device_id_type=MESH,
         )
 
@@ -462,7 +477,7 @@
         cols = pl.ds(n * NW, NW)
         return pltpu.make_async_remote_copy(
             src_ref=sb.at[j - 1, :, cols], dst_ref=fb.at[j - 1, :, cols],
-            send_sem=ys_sem, recv_sem=yr_sem.at[j - 1, n],
+            send_sem=ys_sem, recv_sem=yr_sem.at[j - 1, n // (NO - 1)],
             device_id=(s_id, peer_y(j) * CORES + c), device_id_type=MESH,
         )
 
@@ -503,19 +518,24 @@
 
     lax.fori_loop(0, NP, project_near, 0)
 
-    for n in range(NP):
-        pair_near(n).wait_recv()
+    pltpu.make_async_copy(rb.at[0], rb.at[0], pn_sem).wait()
+
+    def landed(j, n, count):
+        rows = fb.at[j - 1, :, pl.ds(n * NW, count * NW)]
+        pltpu.make_async_copy(rows, rows, yr_sem.at[j - 1, n // (NO - 1)]).wait()
 
     def finish(n, _):
         cols = pl.ds(n * NW, NW)
         total = keep[0, :, cols].astype(F32) + rb[0, :, cols].astype(F32)
         for j in range(1, Y):
-            far_copy(j, n).wait_recv()
             total = total + fb[j - 1, :, cols].astype(F32)
         out[:, cols] = total.astype(BF16)
         return 0
 
-    lax.fori_loop(0, NO, finish, 0)
+    for first, count in ((0, NO - 1), (NO - 1, 1)):
+        for j in range(1, Y):
+            landed(j, first, count)
+        lax.fori_loop(first, first + count, finish, 0)
 
     def drain(ref, sem):
         pltpu.make_async_copy(ref, ref, sem).wait()
@@ -595,7 +615,7 @@
             dma((3,)), dma, dma((2,)), dma, dma,
             dma, dma, dma((far, PARTS)), dma((far, PARTS)),
             dma, dma, dma((Z, 2 + PARTS)), dma((max(1, X - 1), Z, 2 + PARTS)),
-            dma, dma((far, NO)), dma((NP,)), dma, dma((far, NO)),
+            dma, dma((far, NO)), dma, dma, dma((far, 2)),
             pltpu.SemaphoreType.REGULAR((2,)),
         ],
         compiler_params=pltpu.CompilerParams(

time: 47.8 us -> 47.4 us (level)
  no operation moved by 1% of the time
where the time goes in v5:
time: 47.4 us; the launch traced here: 47.3 us
  Pallas kernels  46.5 us (98%)
  local copies, waits for them, and re-layouts  0.8 us (2%)
    pallas_call x1, Pallas kernels, on_device(): pl.pallas_call(functools.partial(kernel, X, Z, Y, PARTS, NO, NP), out_sha...  46.5 us

profile of v5, /device:TPU:0, one launch (start us, length us, event | category | flops | bytes accessed | tf_op | source)
XLA Modules:
  0.0 47.3 jit_solution(1150595567819137092)
XLA Ops:
  0.0 46.5 %shard_map.82 = bf16[64,4096]{1,0:T(8,128)(2,1)S(1)} custom-call(s32[16]{0:T(128)} %order_hbm.1, bf16[64,4096]{1,0:T(8,128)(2,1)} %hidden.1, s32[16,128]{1,0:T(8,128)} %bitcast.1, f32[1,128]{1,0:T(1,128)} %constant.2.clone.freq_hbm, bf16[4096,1024]{1,0:T(8,128)(2,1)} %wq.1, bf16[4096,256]{1,0:T(8,128)(2,1)} %wk.1, bf16[4096,256]{1,0:T(8,128)(2,1)} %wv.1, ...), custom_call_target="tpu_custom_call" | custom-call | tf_op jit(solution)/shard_map/pallas_call | solution.py:591
  46.5 0.8 %copy.10 = bf16[64,4096]{1,0:T(8,128)(2,1)} copy(bf16[64,4096]{1,0:T(8,128)(2,1)S(1)} %shard_map.82) | data formatting | bytes 1048576

commit v6 on v5

--- a/solution.py
+++ b/solution.py
@@ -422,9 +422,6 @@
         hidden_on(e)
         hidden_in(e)
         store_kv(2 + e)
-    for p in F_ALL[:-1]:
-        for way in range(1, X):
-            cross_on(way, p)
     for d in range(Z - 1, 1, -1):
         for p in F_ALL[:-1]:
             relay(d, d + 1, p)
@@ -440,6 +437,9 @@
     relay(3, Z, 1)
     for d in range(Z - 1, 1, -1):
         relay(d, d + 1, 1 + PARTS)
+    for p in F_ALL[:-1]:
+        for way in range(1, X):
+            cross_on(way, p)
     for way in range(1, X):
         cross_on(way, 1 + PARTS)
     relay(1, 2, 1 + PARTS)

time: 47.4 us -> 47.4 us (level)
  no operation moved by 1% of the time
where the time goes in v6:
time: 47.4 us; the launch traced here: 47.3 us
  Pallas kernels  46.5 us (98%)
  local copies, waits for them, and re-layouts  0.8 us (2%)
    pallas_call x1, Pallas kernels, on_device(): pl.pallas_call(functools.partial(kernel, X, Z, Y, PARTS, NO, NP), out_sha...  46.5 us

profile of v6, /device:TPU:0, one launch (start us, length us, event | category | flops | bytes accessed | tf_op | source)
XLA Modules:
  0.0 47.3 jit_solution(11935808735789493990)
XLA Ops:
  0.0 46.5 %shard_map.82 = bf16[64,4096]{1,0:T(8,128)(2,1)S(1)} custom-call(s32[16]{0:T(128)} %order_hbm.1, bf16[64,4096]{1,0:T(8,128)(2,1)} %hidden.1, s32[16,128]{1,0:T(8,128)} %bitcast.1, f32[1,128]{1,0:T(1,128)} %constant.2.clone.freq_hbm, bf16[4096,1024]{1,0:T(8,128)(2,1)} %wq.1, bf16[4096,256]{1,0:T(8,128)(2,1)} %wk.1, bf16[4096,256]{1,0:T(8,128)(2,1)} %wv.1, ...), custom_call_target="tpu_custom_call" | custom-call | tf_op jit(solution)/shard_map/pallas_call | solution.py:591
  46.5 0.8 %copy.10 = bf16[64,4096]{1,0:T(8,128)(2,1)} copy(bf16[64,4096]{1,0:T(8,128)(2,1)S(1)} %shard_map.82) | data formatting | bytes 1048576
